TPU v7x, 32 devices: a whole 2x2x4 slice. The times are simulated.
32 devices in a mesh: groups: 2 (over x), seq: 16 (over z, y, core).
Axes of the slice: x: 2, y: 2, z: 4, core: 2. Of those that a mesh axis runs over, the one named last changes fastest.
Arguments:
- queries: bfloat16 [2048, 24576], P(('groups', 'seq')), parts along dimension 0, may hold values from -500 to 500
- kv_new: bfloat16 [2048, 576], P(('groups', 'seq')), parts along dimension 0, may hold values from -6 to 6
- kv_cache: bfloat16 [1024, 576], P(('groups', 'seq')), parts along dimension 0, may hold values from -6 to 6
- kv_gain: float32 [512], replicated, may hold values from 0.5 to 2
- w_key: bfloat16 [512, 16384], P(None, 'seq'), may hold values from -0.25 to 0.25
- w_value: bfloat16 [512, 16384], P(None, 'seq'), may hold values from -0.25 to 0.25
- prefix_len: int32 [2], P('groups'), parts along dimension 0, may hold values from 128 to 512
Outputs:
- attended: bfloat16 [2048, 16384], P(('groups', 'seq')), parts along dimension 0
There are 2 independent parts, one for each index of `groups`. A program takes and returns all parts, laid end to end along the dimension named above; an argument that names none is the same for every part. Nothing has to cross between parts.
Inputs may be any that keep to these rules, and one draw needn't show every extreme that they name: The stretch's tokens take positions from prefix_len on.
All inputs are finite; a program needn't handle non-finite values.
Results may differ from a plain program's by a relative error of at most 0.012.
Values may be sent and summed in bfloat16 or wider, within the bound.
A program may use at most 128 MiB of HBM per device.

v0:
```python
import functools
import math

import jax
import jax.numpy as jnp
from jax import lax
from jax.experimental import pallas as pl
from jax.experimental.pallas import tpu as pltpu
from jax.sharding import PartitionSpec as P

NOPE = 128
ROPE = 64
LATENT = 512
VH = 128
WIDTH = NOPE + ROPE
INNER = 4

epsilon = 1e-06


def exclusive(a, b, extent):
    result = 0
    bit = 1
    while bit < extent:
        result = result + ((a // bit + b // bit) % 2) * bit
        bit *= 2
    return result


def inverse_lanes():
    half = ROPE // 2
    inverse = 10000.0 ** (-(jnp.arange(half, dtype=jnp.float32) * 2.0) / ROPE)
    return jnp.concatenate([inverse] * 4)[None, :]


def swap_halves(x, lane):
    return jnp.where(lane % ROPE < ROPE // 2, pltpu.roll(x, 96, 1), pltpu.roll(x, 32, 1))


def kernel(
    n, tok, cac, heads, chunks,
    q_hbm, kvn_hbm, kvc_hbm, wk_hbm, wv_hbm, gain_ref, inverse_ref, plen_ref,
    out_hbm,
    qbuf, kvn, kvc, weights, keys, vals, bias, obuf, cos_ref, sin_ref,
    local_sem, own_out_sem, q_send, q_recv, kv_send, kv_recv, o_send, o_recv, w_send, w_recv,
):
    me = lax.axis_index("seq")
    part = lax.axis_index("groups")
    piece = part % 2
    half = n // 2
    mirror = (me + half) % n
    half_first = (me // half) * half
    half_slabs = half // INNER
    slab = me // INNER
    inner = me % INNER
    slabs = n // INNER
    T, C = n * tok, n * cac
    S = T + C
    qw = heads * WIDTH
    ow = heads * VH
    rows = INNER * tok
    f32, bf16 = jnp.float32, jnp.bfloat16

    def blk(ref, b, size):
        return ref.at[pl.ds(pl.multiple_of(b * size, size), size), :]

    def cols(ref, b, size):
        return ref.at[:, pl.ds(pl.multiple_of(b * size, 128), size)]

    own = [
        pltpu.make_async_copy(kvn_hbm, blk(kvn, me, tok), local_sem.at[0]),
        pltpu.make_async_copy(kvc_hbm, blk(kvc, me, cac), local_sem.at[1]),
        pltpu.make_async_copy(wk_hbm, weights.at[0, 0], local_sem.at[2]),
        pltpu.make_async_copy(wv_hbm, weights.at[1, 0], local_sem.at[3]),
        pltpu.make_async_copy(
            cols(q_hbm, me, qw), blk(qbuf.at[0], me - half_first, tok), local_sem.at[4]
        ),
        pltpu.make_async_copy(
            cols(q_hbm, mirror, qw), blk(qbuf.at[1], me - half_first, tok), local_sem.at[5]
        ),
    ]
    for copy in own:
        copy.start()

    barrier = pltpu.get_barrier_semaphore()

    @pl.loop(1, n)
    def _(i):
        pl.semaphore_signal(barrier, inc=1, device_id={"seq": (me + i) % n})

    beside = {"groups": part + 1 - 2 * piece, "seq": me}
    pl.semaphore_signal(barrier, inc=1, device_id=beside)
    pl.semaphore_wait(barrier, n)

    def kv_copies(stage, b, peer, from_hbm):
        slot = b if stage else peer
        return [
            pltpu.make_async_remote_copy(
                src_ref=kvn_hbm if from_hbm else blk(kvn, b, tok),
                dst_ref=blk(kvn, b, tok),
                send_sem=kv_send.at[2 * stage, slot],
                recv_sem=kv_recv.at[0, b],
                device_id={"seq": peer},
            ),
            pltpu.make_async_remote_copy(
                src_ref=kvc_hbm if from_hbm else blk(kvc, b, cac),
                dst_ref=blk(kvc, b, cac),
                send_sem=kv_send.at[2 * stage + 1, slot],
                recv_sem=kv_recv.at[1, b],
                device_id={"seq": peer},
            ),
        ]

    def q_copy(k, peer, source):
        return pltpu.make_async_remote_copy(
            src_ref=cols(q_hbm, (peer + k * half) % n, qw),
            dst_ref=blk(qbuf.at[k], source - half_first, tok),
            send_sem=q_send.at[k, peer],
            recv_sem=q_recv.at[k, source],
            device_id={"seq": peer},
        )

    def o_copy(k, peer, source):
        return pltpu.make_async_remote_copy(
            src_ref=blk(obuf.at[k], peer - half_first, tok),
            dst_ref=cols(out_hbm, (source + k * half) % n, ow),
            send_sem=o_send.at[k, peer],
            recv_sem=o_recv.at[k, source],
            device_id={"seq": peer},
        )

    def own_out(k):
        return pltpu.make_async_copy(
            blk(obuf.at[k], me - half_first, tok),
            cols(out_hbm, (me + k * half) % n, ow),
            own_out_sem.at[k],
        )

    deep = LATENT // chunks

    def w_chunk(which, k, i):
        return weights.at[which, k, pl.ds(pl.multiple_of(i * deep, deep), deep), :]

    def w_direct(i):
        return pltpu.make_async_remote_copy(
            src_ref=w_chunk(piece, 0, i),
            dst_ref=w_chunk(piece, 1, i),
            send_sem=w_send.at[0, i],
            recv_sem=w_recv.at[0, i],
            device_id={"seq": mirror},
        )

    def w_beside(which, i):
        return pltpu.make_async_remote_copy(
            src_ref=w_chunk(which, 1, i),
            dst_ref=w_chunk(which, 1, i),
            send_sem=w_send.at[1, i],
            recv_sem=w_recv.at[1, i],
            device_id=beside,
        )

    @pl.loop(1, slabs)
    def _(j):
        for copy in kv_copies(0, me, exclusive(slab, j, slabs) * INNER + inner, True):
            copy.start()

    near = (inner // 2) * 2
    far = (near + 2) % INNER

    def q_near(k):
        @pl.loop(1, half_slabs)
        def _(j):
            other = exclusive(slab, j, slabs) * INNER
            for c in range(2):
                q_copy(k, other + near + c, me).start()

    def q_slab(k):
        @pl.loop(1, INNER)
        def _(i):
            q_copy(k, slab * INNER + (inner + i) % INNER, me).start()

    def q_far(k):
        @pl.loop(1, half_slabs)
        def _(j):
            other = exclusive(slab, j, slabs) * INNER
            for c in range(2):
                q_copy(k, other + far + c, me).start()

    q_near(0)

    across = slab * INNER + (inner + 2) % INNER
    twin = me + 1 - 2 * (me % 2)
    own[0].wait()
    own[1].wait()

    @pl.loop(0, slabs)
    def _(j):
        b = exclusive(slab, j, slabs) * INNER + inner

        @pl.when(j > 0)
        def _():
            for copy in kv_copies(0, b, twin, False):
                copy.wait_recv()

        for copy in kv_copies(1, b, across, False):
            copy.start()
        for copy in kv_copies(2, b, twin, False):
            copy.start()

    q_slab(0)

    @pl.loop(0, slabs)
    def _(j):
        b = exclusive(slab, j, slabs) * INNER + (inner + 2) % INNER
        for copy in kv_copies(1, b, twin, False):
            copy.wait_recv()
        for copy in kv_copies(2, b, twin, False):
            copy.start()

    q_far(0)
    own[2].wait()
    own[3].wait()

    @pl.loop(0, chunks)
    def _(i):
        w_direct(i).start()

    q_near(1)
    q_slab(1)
    q_far(1)

    csize = math.gcd(C, 256)
    tsize = math.gcd(T, 256)

    @pl.loop(0, T // tsize)
    def _(i):
        first = pl.multiple_of(i * tsize, tsize)
        at = pl.ds(first, tsize)
        lane = lax.broadcasted_iota(jnp.int32, (tsize, 128), 1)
        position = plen_ref[0] + first + lax.broadcasted_iota(jnp.int32, (tsize, 128), 0)
        phase = position.astype(f32) * inverse_ref[...]
        cos_ref[at, :] = jnp.cos(phase)
        sine = jnp.sin(phase)
        sin_ref[at, :] = jnp.where(lane % ROPE < ROPE // 2, -sine, sine)

    @pl.loop(0, slabs)
    def _(j):
        for k in range(2):
            b = exclusive(slab, j, slabs) * INNER + (twin + 2 * k) % INNER
            for copy in kv_copies(2, b, twin, False):
                copy.wait_recv()

    own[4].wait()
    own[5].wait()

    def project(k, latent, rope, first, size):
        lane = lax.broadcasted_iota(jnp.int32, (size, 128), 1)
        at = pl.ds(first, size)
        rope_even = jnp.where(lane < ROPE, rope, 0.0).astype(bf16)
        for h in range(0, heads, 2):
            pair = jnp.dot(latent, weights[0, k, :, h * NOPE : (h + 2) * NOPE], preferred_element_type=f32)
            keys[h, at, 0:128] = pair[:, :128].astype(bf16)
            keys[h, at, 128:256] = rope_even
            turned = pltpu.roll(pair[:, 128:], 64, 1)
            keys[h + 1, at, 0:128] = jnp.where(lane < ROPE, 0.0, turned).astype(bf16)
            keys[h + 1, at, 128:256] = jnp.where(lane < ROPE, turned, rope).astype(bf16)
            vals[at, h * VH : (h + 2) * VH] = jnp.dot(
                latent, weights[1, k, :, h * VH : (h + 2) * VH], preferred_element_type=f32
            ).astype(bf16)

    scale = math.log2(math.e) / math.sqrt(WIDTH)
    per_slab = chunks // half_slabs

    @pl.loop(0, 2)
    def _(k):
        @pl.when(k == 1)
        def _():
            @pl.loop(0, chunks)
            def _(i):
                w_beside(1 - piece, i).wait_recv()

        @pl.loop(0, C // csize)
        def _(i):
            first = pl.multiple_of(i * csize, csize)
            raw = kvc[pl.ds(first, csize), :]
            rope = raw[:, LATENT:].astype(f32)
            project(k, raw[:, :LATENT], jnp.concatenate([rope, rope], 1), first, csize)

        @pl.loop(0, T // tsize)
        def _(i):
            first = pl.multiple_of(i * tsize, tsize)
            at = pl.ds(first, tsize)
            raw = kvn[at, :]
            wide = raw[:, :LATENT].astype(f32)
            inv = lax.rsqrt(jnp.mean(wide * wide, axis=1, keepdims=True) + epsilon)
            latent = (wide * inv * gain_ref[...]).astype(bf16)
            rope = raw[:, LATENT:].astype(f32)
            rope = jnp.concatenate([rope, rope], 1)
            lane = lax.broadcasted_iota(jnp.int32, (tsize, 128), 1)
            rope = rope * cos_ref[at, :] + swap_halves(rope, lane) * sin_ref[at, :]
            project(k, latent, rope, pl.multiple_of(C + first, tsize), tsize)

        @pl.loop(0, half_slabs)
        def _(j):
            group = exclusive(slab, j + k * (half_slabs - 1 - 2 * j), slabs)

            @pl.loop(0, INNER)
            def _(i):
                b = group * INNER + i

                @pl.when(b != me)
                def _():
                    q_copy(k, me, b).wait_recv()

            base = pl.multiple_of(group * rows, rows)
            at = pl.ds(base, rows)
            near_at = pl.ds(pl.multiple_of(base - half_first * tok, rows), rows)
            row = base + lax.broadcasted_iota(jnp.int32, (rows, S), 0)
            col = lax.broadcasted_iota(jnp.int32, (rows, S), 1)
            live = ((col < C) & (col < plen_ref[0])) | ((col >= C) & (col - C <= row))
            bias[...] = jnp.where(live, 0.0, -1e30)

            @pl.loop(0, heads // 2)
            def _(p):
                lane = lax.broadcasted_iota(jnp.int32, (rows, 128), 1)
                cosine = cos_ref[at, :]
                sine = sin_ref[at, :]

                def third(i):
                    return qbuf[k, near_at, pl.ds(pl.multiple_of(p * 384 + 128 * i, 128), 128)]

                def turn(x, hit):
                    x = x.astype(f32)
                    y = x * cosine + swap_halves(x, lane) * sine
                    return jnp.where(hit, y, x).astype(bf16)

                front = third(0)
                middle = turn(third(1), lane < ROPE)
                back = turn(third(2), lane >= ROPE)
                for side, query in enumerate(
                    (jnp.concatenate([front, middle], 1), jnp.concatenate([middle, back], 1))
                ):
                    h = 2 * p + side
                    scores = lax.dot_general(
                        query, keys[h], (((1,), (1,)), ((), ())), preferred_element_type=f32
                    )
                    scores = scores * scale + bias[...]
                    top = jnp.max(scores, axis=1, keepdims=True)
                    grown = jnp.exp2(scores - top)
                    total = jnp.sum(grown, axis=1, keepdims=True)
                    across_v = pl.ds(pl.multiple_of(h * VH, VH), VH)
                    mixed = jnp.dot(grown.astype(bf16), vals[:, across_v], preferred_element_type=f32)
                    obuf[k, near_at, across_v] = (mixed / total).astype(bf16)

            @pl.loop(0, INNER)
            def _(i):
                b = group * INNER + i

                @pl.when(b != me)
                def _():
                    o_copy(k, b, me).start()

                @pl.when(b == me)
                def _():
                    own_out(k).start()

            @pl.when(k == 0)
            def _():
                @pl.loop(j * per_slab, (j + 1) * per_slab)
                def _(i):
                    w_direct(i).wait_recv()
                    w_beside(piece, i).start()

    for k in range(2):
        own_out(k).wait()

        @pl.loop(1, half)
        def _(i):
            peer = half_first + (me + i) % half
            q_copy(k, peer, me).wait_send()
            o_copy(k, peer, me).wait_send()
            o_copy(k, me, peer).wait_recv()

    @pl.loop(0, chunks)
    def _(i):
        w_direct(i).wait_send()
        w_beside(piece, i).wait_send()

    @pl.loop(0, slabs)
    def _(j):
        b = exclusive(slab, j, slabs) * INNER + inner

        @pl.when(j > 0)
        def _():
            for copy in kv_copies(0, me, b, True):
                copy.wait_send()

        for copy in kv_copies(1, b, across, False):
            copy.wait_send()
        for k in range(2):
            d = exclusive(slab, j, slabs) * INNER + (inner + 2 * k) % INNER
            for copy in kv_copies(2, d, twin, False):
                copy.wait_send()


def local(n, queries, kv_new, kv_cache, kv_gain, w_key, w_value, prefix_len):
    tok = queries.shape[0]
    cac = kv_cache.shape[0]
    heads = w_key.shape[1] // NOPE
    T, C = n * tok, n * cac
    chunks = max(4, n // (2 * INNER))
    hbm = pl.BlockSpec(memory_space=pl.ANY)
    vmem = pl.BlockSpec(memory_space=pltpu.VMEM)
    bf16 = jnp.bfloat16
    dma = pltpu.SemaphoreType.DMA
    return pl.pallas_call(
        functools.partial(kernel, n, tok, cac, heads, chunks),
        out_shape=jax.ShapeDtypeStruct((tok, n * heads * VH), bf16),
        in_specs=[hbm] * 5 + [vmem] * 2 + [pl.BlockSpec(memory_space=pltpu.SMEM)],
        out_specs=hbm,
        scratch_shapes=[
            pltpu.VMEM((2, T // 2, heads * WIDTH), bf16),
            pltpu.VMEM((T, LATENT + ROPE), bf16),
            pltpu.VMEM((C, LATENT + ROPE), bf16),
            pltpu.VMEM((2, 2, LATENT, heads * NOPE), bf16),
            pltpu.VMEM((heads, C + T, 256), bf16),
            pltpu.VMEM((C + T, heads * VH), bf16),
            pltpu.VMEM((INNER * tok, C + T), jnp.float32),
            pltpu.VMEM((2, T // 2, heads * VH), bf16),
            pltpu.VMEM((T, 128), jnp.float32),
            pltpu.VMEM((T, 128), jnp.float32),
            dma((6,)),
            dma((2,)),
            dma((2, n)),
            dma((2, n)),
            dma((6, n)),
            dma((2, n)),
            dma((2, n)),
            dma((2, n)),
            dma((2, chunks)),
            dma((2, chunks)),
        ],
        compiler_params=pltpu.CompilerParams(
            collective_id=0, has_side_effects=True, vmem_limit_bytes=60 * 2**20
        ),
        name="latent_attention",
    )(queries, kv_new, kv_cache, w_key, w_value, kv_gain[None, :], inverse_lanes(), prefix_len)


def solution(mesh):
    placed = (
        P(("groups", "seq"), None),
        P(("groups", "seq"), None),
        P(("groups", "seq"), None),
        P(),
        P(None, "seq"),
        P(None, "seq"),
        P("groups"),
    )
    return jax.shard_map(
        functools.partial(local, mesh.shape["seq"]),
        mesh=mesh,
        in_specs=placed,
        out_specs=P(("groups", "seq"), None),
        check_vma=False,
    )
```

profile of v0, /device:TPU:1, one launch (start us, length us, event | category | flops | bytes accessed | tf_op | source)
XLA Modules:
  0.0 108.3 jit_solution(5587064150160573907)
XLA Ops:
  0.7 0.6 maximum_bitcast_fusion.inverse_ref
  1.3 104.0 %latent_attention.1 = bf16[64,16384]{1,0:T(8,128)(2,1)} custom-call(bf16[64,24576]{1,0:T(8,128)(2,1)} %q_hbm.1, bf16[64,576]{1,0:T(8,128)(2,1)} %kvn_hbm.1, bf16[32,576]{1,0:T(8,128)(2,1)} %kvc_hbm.1, bf16[512,1024]{1,0:T(8,128)(2,1)} %wk_hbm.1, bf16[512,1024]{1,0:T(8,128)(2,1)} %wv_hbm.1, f32[1,512]{1,0:T(1,128)} %bitcast.3, ...), custom_call_target="tpu_custom_call" | custom-call | tf_op jit(solution)/shard_map/latent_attention/pallas_call | solution.py:416
  105.3 3.0 %copy.10 = bf16[64,16384]{1,0:T(8,128)(2,1)} copy(bf16[64,16384]{1,0:T(8,128)(2,1)} %latent_attention.1) | data formatting | bytes 4194304
  (1 shorter events, 0.0 us)
where the time goes:
time: 108 us
  Pallas kernels  104 us (96%)
  local copies, waits for them, and re-layouts  3.05 us (3%)
    pallas_call x1, Pallas kernels, local(): pl.pallas_call(functools.partial(kernel, n, tok, cac, heads, chunks), out...  104 us
    unnamed x1, local copies, waits for them, and re-layouts  3.05 us

commit v1 on v0

--- a/solution.py
+++ b/solution.py
@@ -403,7 +403,500 @@
                 copy.wait_send()
 
 
-def local(n, queries, kv_new, kv_cache, kv_gain, w_key, w_value, prefix_len):
+PLANES = 4
+EXTRA_END = 2
+EXTRA_MIDDLE = 1
+
+
+def planes_kernel(
+    n, tok, cac, heads,
+    q_hbm, kvn_hbm, kvc_hbm, wk_hbm, wv_hbm, gain_ref, inverse_ref, plen_ref,
+    out_hbm,
+    qbuf, kvn, kvc, weights, latents, aux, keys, vals, bias, score_a, score_b, prob_a, prob_b, obuf,
+    cos_ref, sin_ref,
+    local_sem, own_q_sem, own_out_sem, q_send, q_recv, kv_send, kv_recv, o_send, o_recv, w_send, w_recv,
+):
+    me = lax.axis_index("seq")
+    part = lax.axis_index("groups")
+    piece = part % 2
+    plane = me // INNER
+    inner = me % INNER
+    side = plane // (PLANES // 2)
+    last = PLANES - 1
+
+    def whole(r):
+        return r + side * (last - 2 * r)
+
+    middle = whole(plane)
+    end = middle == 0
+    mid = middle == 1
+    T, C = n * tok, n * cac
+    S = T + C
+    qw = heads * WIDTH
+    ow = heads * VH
+    rows = INNER * tok
+    pairs = heads // 2
+    f32, bf16 = jnp.float32, jnp.bfloat16
+    scale = math.log2(math.e) / math.sqrt(WIDTH)
+
+    def blk(ref, b, size):
+        return ref.at[pl.ds(pl.multiple_of(b * size, size), size), :]
+
+    def cols(ref, b, size):
+        return ref.at[:, pl.ds(pl.multiple_of(b * size, 128), size)]
+
+    def head_plane(k):
+        return whole(jnp.where(end, k, jnp.where(k == 0, 1, jnp.where(k == 1, 0, k))))
+
+    steps = 3 + middle
+
+    def own_q(k):
+        return pltpu.make_async_copy(
+            cols(q_hbm, head_plane(k) * INNER + inner, qw), blk(qbuf.at[k], inner, tok), own_q_sem.at[k]
+        )
+
+    own = [
+        pltpu.make_async_copy(kvn_hbm, blk(kvn, me, tok), local_sem.at[0]),
+        pltpu.make_async_copy(kvc_hbm, blk(kvc, me, cac), local_sem.at[1]),
+        pltpu.make_async_copy(wk_hbm, weights.at[0, 0], local_sem.at[2]),
+        pltpu.make_async_copy(wv_hbm, weights.at[0, 1], local_sem.at[3]),
+    ]
+    for copy in own:
+        copy.start()
+
+    barrier = pltpu.get_barrier_semaphore()
+
+    @pl.loop(1, n)
+    def _(i):
+        pl.semaphore_signal(barrier, inc=1, device_id={"seq": (me + i) % n})
+
+    beside = {"groups": part + 1 - 2 * piece, "seq": me}
+    pl.semaphore_signal(barrier, inc=1, device_id=beside)
+    pl.semaphore_wait(barrier, n)
+
+    def kv_copies(stage, b, peer, from_hbm):
+        slot = b if stage else peer
+        return [
+            pltpu.make_async_remote_copy(
+                src_ref=kvn_hbm if from_hbm else blk(kvn, b, tok),
+                dst_ref=blk(kvn, b, tok),
+                send_sem=kv_send.at[2 * stage, slot],
+                recv_sem=kv_recv.at[0, b],
+                device_id={"seq": peer},
+            ),
+            pltpu.make_async_remote_copy(
+                src_ref=kvc_hbm if from_hbm else blk(kvc, b, cac),
+                dst_ref=blk(kvc, b, cac),
+                send_sem=kv_send.at[2 * stage + 1, slot],
+                recv_sem=kv_recv.at[1, b],
+                device_id={"seq": peer},
+            ),
+        ]
+
+    def q_copy(k, to_plane, to, source):
+        columns = jnp.where(k == PLANES, whole(last), head_plane(k)) * INNER + to
+        return pltpu.make_async_remote_copy(
+            src_ref=cols(q_hbm, columns, qw),
+            dst_ref=blk(qbuf.at[k], source, tok),
+            send_sem=q_send.at[k, to],
+            recv_sem=q_recv.at[k, source],
+            device_id={"seq": to_plane * INNER + to},
+        )
+
+    def o_copy(k, to_plane, to, source):
+        columns = jnp.where(k == PLANES, whole(last), head_plane(k)) * INNER + source
+        return pltpu.make_async_remote_copy(
+            src_ref=blk(obuf.at[k], to, tok),
+            dst_ref=cols(out_hbm, columns, ow),
+            send_sem=o_send.at[k, to],
+            recv_sem=o_recv.at[k, source],
+            device_id={"seq": to_plane * INNER + to},
+        )
+
+    def own_out(k):
+        return pltpu.make_async_copy(
+            blk(obuf.at[k], inner, tok), cols(out_hbm, head_plane(k) * INNER + inner, ow), own_out_sem.at[k]
+        )
+
+    def w_chunk(k, which, i):
+        return weights.at[k, which, :, pl.ds(pl.multiple_of(i * 2 * NOPE, 128), 2 * NOPE)]
+
+    def w_copy(way, k, to_k, which, i, device):
+        return pltpu.make_async_remote_copy(
+            src_ref=w_chunk(k, which, i),
+            dst_ref=w_chunk(to_k, which, i),
+            send_sem=w_send.at[way, k, which, i],
+            recv_sem=w_recv.at[to_k, which, i],
+            device_id=device,
+        )
+
+    near = {"seq": whole(1 - middle) * INNER + inner}
+    beyond = {"seq": whole(2) * INNER + inner}
+
+    def w_near(k, which, i):
+        return w_copy(0, k, jnp.where(k == 0, 1, 2), which, i, near)
+
+    def w_beyond(k, which, i):
+        return w_copy(1, k, k + 2, which, i, beyond)
+
+    def w_beside(k, i):
+        return w_copy(2, k, k, piece, i, beside)
+
+    def extras(k):
+        return jnp.where(mid, jnp.where(k == 1, EXTRA_END, jnp.where(k == 2, EXTRA_MIDDLE, 0)), 0)
+
+    def for_own_weights(do):
+        @pl.loop(0, pairs)
+        def _(i):
+            do(w_near(0, piece, i))
+
+            @pl.when(mid)
+            def _():
+                do(w_beyond(0, piece, i))
+
+        @pl.when(end)
+        def _():
+            @pl.loop(pairs - EXTRA_END, pairs)
+            def _(i):
+                do(w_near(0, 1 - piece, i))
+
+        @pl.when(mid)
+        def _():
+            @pl.loop(pairs - EXTRA_MIDDLE, pairs)
+            def _(i):
+                do(w_beyond(0, 1 - piece, i))
+
+    def for_forwards(k, i, do):
+        @pl.when(mid & (k == 1))
+        def _():
+            do(w_beyond(k, piece, i))
+
+        @pl.when(mid & (k == 2))
+        def _():
+            do(w_near(k, piece, i))
+
+        @pl.when(i < pairs - extras(k))
+        def _():
+            do(w_beside(k, i))
+
+    def pass_on(k, i):
+        w_copy(2, k, k, piece, i, beside).wait_recv()
+        for_forwards(k, i, lambda copy: copy.start())
+
+    @pl.loop(1, PLANES)
+    def _(j):
+        for copy in kv_copies(0, me, exclusive(plane, j, PLANES) * INNER + inner, True):
+            copy.start()
+
+    own[2].wait()
+    own[3].wait()
+    for_own_weights(lambda copy: copy.start())
+
+    across = plane * INNER + (inner + 2) % INNER
+    twin = me + 1 - 2 * (me % 2)
+    own[0].wait()
+    own[1].wait()
+
+    @pl.loop(0, steps)
+    def _(k):
+        own_q(k).start()
+
+    @pl.loop(0, PLANES)
+    def _(j):
+        b = exclusive(plane, j, PLANES) * INNER + inner
+
+        @pl.when(j > 0)
+        def _():
+            for copy in kv_copies(0, b, twin, False):
+                copy.wait_recv()
+
+        for copy in kv_copies(1, b, across, False):
+            copy.start()
+        for copy in kv_copies(2, b, twin, False):
+            copy.start()
+
+    def for_queries(k, do):
+        @pl.loop(1, INNER)
+        def _(i):
+            do(q_copy(k, plane, (inner + i) % INNER, inner))
+
+    for_queries(0, lambda copy: copy.start())
+
+    tsize = math.gcd(T, 256)
+    csize = math.gcd(C, 256)
+
+    @pl.loop(0, T // tsize)
+    def _(i):
+        first = pl.multiple_of(i * tsize, tsize)
+        at = pl.ds(first, tsize)
+        lane = lax.broadcasted_iota(jnp.int32, (tsize, 128), 1)
+        position = plen_ref[0] + first + lax.broadcasted_iota(jnp.int32, (tsize, 128), 0)
+        phase = position.astype(f32) * inverse_ref[...]
+        cos_ref[at, :] = jnp.cos(phase)
+        sine = jnp.sin(phase)
+        sin_ref[at, :] = jnp.where(lane % ROPE < ROPE // 2, -sine, sine)
+
+    bias[...] = jnp.where(
+        lax.broadcasted_iota(jnp.int32, (rows, rows), 1) <= lax.broadcasted_iota(jnp.int32, (rows, rows), 0),
+        0.0, -1e30,
+    )
+
+    @pl.loop(0, PLANES)
+    def _(j):
+        b = exclusive(plane, j, PLANES) * INNER + (inner + 2) % INNER
+        for copy in kv_copies(1, b, twin, False):
+            copy.wait_recv()
+        for copy in kv_copies(2, b, twin, False):
+            copy.start()
+
+    @pl.loop(1, steps)
+    def _(k):
+        for_queries(k, lambda copy: copy.start())
+
+    def for_far_queries(do):
+        @pl.loop(0, INNER)
+        def _(i):
+            do(q_copy(PLANES, whole(1), (inner + i) % INNER, inner))
+
+    @pl.when(end)
+    def _():
+        for_far_queries(lambda copy: copy.start())
+
+    @pl.loop(0, heads)
+    def _(h):
+        vals[h, :, 128:256] = jnp.ones((S, 128), bf16)
+
+    @pl.loop(0, PLANES)
+    def _(j):
+        for k in range(2):
+            b = exclusive(plane, j, PLANES) * INNER + (twin + 2 * k) % INNER
+            for copy in kv_copies(2, b, twin, False):
+                copy.wait_recv()
+
+    def keep_rope(first, size, rope, dead):
+        at = pl.ds(first, size)
+        lane = lax.broadcasted_iota(jnp.int32, (size, 128), 1)
+        low = lane < ROPE
+        aux[at, :] = jnp.where(low, jnp.where(lane == 0, dead, 0.0), rope)
+        tail = jnp.where(low, rope, jnp.where(lane == ROPE, dead, 0.0)).astype(bf16)
+        for h in range(0, heads, 2):
+            keys[h, at, 128:256] = tail
+
+    @pl.loop(0, C // csize)
+    def _(i):
+        first = pl.multiple_of(i * csize, csize)
+        raw = kvc[pl.ds(first, csize), :]
+        latents[pl.ds(first, csize), :] = raw[:, :LATENT]
+        rope = raw[:, LATENT:].astype(f32)
+        row = first + lax.broadcasted_iota(jnp.int32, (csize, 128), 0)
+        dead = jnp.where(row < plen_ref[0], 0.0, -1e30)
+        keep_rope(first, csize, jnp.concatenate([rope, rope], 1), dead)
+
+    @pl.loop(0, T // tsize)
+    def _(i):
+        first = pl.multiple_of(i * tsize, tsize)
+        at = pl.ds(first, tsize)
+        raw = kvn[at, :]
+        wide = raw[:, :LATENT].astype(f32)
+        inv = lax.rsqrt(jnp.mean(wide * wide, axis=1, keepdims=True) + epsilon)
+        latents[pl.ds(pl.multiple_of(C + first, tsize), tsize), :] = (wide * inv * gain_ref[...]).astype(bf16)
+        rope = raw[:, LATENT:].astype(f32)
+        rope = jnp.concatenate([rope, rope], 1)
+        lane = lax.broadcasted_iota(jnp.int32, (tsize, 128), 1)
+        rope = rope * cos_ref[at, :] + swap_halves(rope, lane) * sin_ref[at, :]
+        keep_rope(pl.multiple_of(C + first, tsize), tsize, rope, 0.0)
+        cos_ref[at, :] = cos_ref[at, :] * scale
+        sin_ref[at, :] = sin_ref[at, :] * scale
+
+    size = math.gcd(C, rows)
+
+    def project(k, p):
+        across_k = pl.ds(pl.multiple_of(p * 2 * NOPE, 128), 2 * NOPE)
+        across_v = pl.ds(pl.multiple_of(p * 2 * VH, 128), 2 * VH)
+
+        top_plane = jnp.where(mid & (k == last), jnp.maximum(plane, whole(0)), plane)
+
+        @pl.loop(0, (C + (top_plane + 1) * rows) // size)
+        def _(i):
+            at = pl.ds(pl.multiple_of(i * size, size), size)
+            latent = latents[at, :]
+            rest = aux[at, :]
+            lane = lax.broadcasted_iota(jnp.int32, (size, 128), 1)
+            pair = jnp.dot(latent, weights[k, 0, :, across_k], preferred_element_type=f32) * scale
+            keys[2 * p, at, 0:128] = pair[:, :128].astype(bf16)
+            turned = pltpu.roll(pair[:, 128:], 64, 1)
+            keys[2 * p + 1, at, 0:128] = jnp.where(lane < ROPE, rest, turned).astype(bf16)
+            keys[2 * p + 1, at, 128:256] = jnp.where(lane < ROPE, turned, rest).astype(bf16)
+            both = jnp.dot(latent, weights[k, 1, :, across_v], preferred_element_type=f32).astype(bf16)
+            vals[2 * p, at, 0:128] = both[:, :128]
+            vals[2 * p + 1, at, 0:128] = both[:, 128:]
+
+    def attend(slot, first_row, live):
+        cut = live - rows
+
+        def rotated(p):
+            at = pl.ds(first_row, rows)
+            lane = lax.broadcasted_iota(jnp.int32, (rows, 128), 1)
+            cosine = cos_ref[at, :]
+            sine = sin_ref[at, :]
+
+            def third(i):
+                return qbuf[slot, :, pl.ds(pl.multiple_of(p * 3 * 128 + 128 * i, 128), 128)]
+
+            def turn(x, hit):
+                x = x.astype(f32)
+                y = x * cosine + swap_halves(x, lane) * sine
+                return jnp.where(hit, y, x)
+
+            centre = turn(third(1), lane < ROPE)
+            return (
+                jnp.concatenate([third(0), jnp.where(lane == ROPE, 1.0, centre).astype(bf16)], 1),
+                jnp.concatenate(
+                    [jnp.where(lane == 0, 1.0, centre).astype(bf16), turn(third(2), lane >= ROPE).astype(bf16)], 1
+                ),
+            )
+
+        def score(query, h, into):
+            into[:, 0:live] = lax.dot_general(
+                query, keys[h, 0:live, :], (((1,), (1,)), ((), ())), preferred_element_type=f32
+            )
+
+        def soften(scores, into):
+            for r in range(0, rows, 16):
+                before = scores[r : r + 16, 0:cut]
+                near_end = scores[r : r + 16, cut:live] + bias[r : r + 16, :]
+                top = jnp.maximum(
+                    jnp.max(before, axis=1, keepdims=True), jnp.max(near_end, axis=1, keepdims=True)
+                )
+                into[r : r + 16, 0:cut] = jnp.exp2(before - top).astype(bf16)
+                into[r : r + 16, cut:live] = jnp.exp2(near_end - top).astype(bf16)
+
+        def mix(probs, h):
+            mixed = jnp.dot(probs[:, 0:live], vals[h, 0:live, :], preferred_element_type=f32)
+            obuf[slot, :, pl.ds(pl.multiple_of(h * VH, VH), VH)] = (mixed[:, :VH] / mixed[:, VH:]).astype(bf16)
+
+        @pl.loop(0, pairs + 1)
+        def _(t):
+            p = jnp.minimum(t, pairs - 1)
+            done = jnp.maximum(t - 1, 0)
+            even, odd = rotated(p)
+            score(even, 2 * p, score_a)
+            soften(score_b, prob_b)
+            mix(prob_a, 2 * done)
+            soften(score_a, prob_a)
+            mix(prob_b, 2 * done + 1)
+            score(odd, 2 * p + 1, score_b)
+
+    @pl.loop(0, steps)
+    def _(k):
+        far = mid & (k == last)
+
+        @pl.loop(0, pairs)
+        def _(p):
+            @pl.when(k > 0)
+            def _():
+                @pl.when((k == 1) | (end & (k == 2)) | ((k == 3) & (p >= 2)))
+                def _():
+                    pass_on(k, p)
+
+                @pl.when(mid & (k == 1))
+                def _():
+                    pass_on(2, p)
+
+                w_copy(2, k, k, 1 - piece, p, beside).wait_recv()
+
+            project(k, p)
+
+        @pl.when(mid & (k == 2))
+        def _():
+            pass_on(3, 0)
+            pass_on(3, 1)
+
+        own_q(k).wait()
+
+        @pl.loop(1, INNER)
+        def _(i):
+            q_copy(k, plane, inner, (inner + i) % INNER).wait_recv()
+
+        for s in range(PLANES):
+            @pl.when(plane == s)
+            def _():
+                attend(k, s * rows, C + (s + 1) * rows)
+
+        own_out(k).start()
+
+        @pl.loop(1, INNER)
+        def _(i):
+            o_copy(k, plane, (inner + i) % INNER, inner).start()
+
+        @pl.when(far)
+        def _():
+            @pl.loop(0, INNER)
+            def _(i):
+                q_copy(PLANES, plane, inner, i).wait_recv()
+
+    for s in range(PLANES):
+        @pl.when(mid & (whole(0) == s))
+        def _():
+            attend(PLANES, s * rows, C + (s + 1) * rows)
+
+    def for_far_outputs(do):
+        @pl.loop(0, INNER)
+        def _(i):
+            do(o_copy(PLANES, whole(0), (inner + i) % INNER, inner))
+
+    @pl.when(mid)
+    def _():
+        for_far_outputs(lambda copy: copy.start())
+
+    @pl.loop(0, steps)
+    def _(k):
+        own_out(k).wait()
+        for_queries(k, lambda copy: copy.wait_send())
+
+        @pl.loop(1, INNER)
+        def _(i):
+            o_copy(k, plane, (inner + i) % INNER, inner).wait_send()
+            o_copy(k, plane, inner, (inner + i) % INNER).wait_recv()
+
+    @pl.when(mid)
+    def _():
+        for_far_outputs(lambda copy: copy.wait_send())
+
+    @pl.when(end)
+    def _():
+        for_far_queries(lambda copy: copy.wait_send())
+
+        @pl.loop(0, INNER)
+        def _(i):
+            o_copy(PLANES, plane, inner, i).wait_recv()
+
+    for_own_weights(lambda copy: copy.wait_send())
+
+    @pl.loop(1, steps)
+    def _(k):
+        @pl.loop(0, pairs)
+        def _(i):
+            for_forwards(k, i, lambda copy: copy.wait_send())
+
+    @pl.loop(0, PLANES)
+    def _(j):
+        b = exclusive(plane, j, PLANES) * INNER + inner
+
+        @pl.when(j > 0)
+        def _():
+            for copy in kv_copies(0, me, b, True):
+                copy.wait_send()
+
+        for copy in kv_copies(1, b, across, False):
+            copy.wait_send()
+        for k in range(2):
+            d = exclusive(plane, j, PLANES) * INNER + (inner + 2 * k) % INNER
+            for copy in kv_copies(2, d, twin, False):
+                copy.wait_send()
+
+
+def local_any(n, queries, kv_new, kv_cache, kv_gain, w_key, w_value, prefix_len):
     tok = queries.shape[0]
     cac = kv_cache.shape[0]
     heads = w_key.shape[1] // NOPE
@@ -447,6 +940,64 @@
     )(queries, kv_new, kv_cache, w_key, w_value, kv_gain[None, :], inverse_lanes(), prefix_len)
 
 
+def local_planes(n, queries, kv_new, kv_cache, kv_gain, w_key, w_value, prefix_len):
+    tok = queries.shape[0]
+    cac = kv_cache.shape[0]
+    heads = w_key.shape[1] // NOPE
+    T, C = n * tok, n * cac
+    S = T + C
+    rows = INNER * tok
+    pairs = heads // 2
+    hbm = pl.BlockSpec(memory_space=pl.ANY)
+    vmem = pl.BlockSpec(memory_space=pltpu.VMEM)
+    bf16, f32 = jnp.bfloat16, jnp.float32
+    dma = pltpu.SemaphoreType.DMA
+    return pl.pallas_call(
+        functools.partial(planes_kernel, n, tok, cac, heads),
+        out_shape=jax.ShapeDtypeStruct((tok, n * heads * VH), bf16),
+        in_specs=[hbm] * 5 + [vmem] * 2 + [pl.BlockSpec(memory_space=pltpu.SMEM)],
+        out_specs=hbm,
+        scratch_shapes=[
+            pltpu.VMEM((PLANES + 1, rows, heads * WIDTH), bf16),
+            pltpu.VMEM((T, LATENT + ROPE), bf16),
+            pltpu.VMEM((C, LATENT + ROPE), bf16),
+            pltpu.VMEM((PLANES, 2, LATENT, heads * NOPE), bf16),
+            pltpu.VMEM((S, LATENT), bf16),
+            pltpu.VMEM((S, 128), f32),
+            pltpu.VMEM((heads, S, 256), bf16),
+            pltpu.VMEM((heads, S, 256), bf16),
+            pltpu.VMEM((rows, rows), f32),
+            pltpu.VMEM((rows, S), f32),
+            pltpu.VMEM((rows, S), f32),
+            pltpu.VMEM((rows, S), bf16),
+            pltpu.VMEM((rows, S), bf16),
+            pltpu.VMEM((PLANES + 1, rows, heads * VH), bf16),
+            pltpu.VMEM((T, 128), f32),
+            pltpu.VMEM((T, 128), f32),
+            dma((4,)),
+            dma((PLANES,)),
+            dma((PLANES,)),
+            dma((PLANES + 1, INNER)),
+            dma((PLANES + 1, INNER)),
+            dma((6, n)),
+            dma((2, n)),
+            dma((PLANES + 1, INNER)),
+            dma((PLANES + 1, INNER)),
+            dma((3, PLANES, 2, pairs)),
+            dma((PLANES, 2, pairs)),
+        ],
+        compiler_params=pltpu.CompilerParams(
+            collective_id=0, has_side_effects=True, vmem_limit_bytes=60 * 2**20
+        ),
+        name="latent_attention",
+    )(queries, kv_new, kv_cache, w_key, w_value, kv_gain[None, :], inverse_lanes(), prefix_len)
+
+
+def local(n, *operands):
+    run = local_planes if n == PLANES * INNER else local_any
+    return run(n, *operands)
+
+
 def solution(mesh):
     placed = (
         P(("groups", "seq"), None),

time: 108 us -> 142 us (1.31)
  the two profiles are of different devices: /device:TPU:1 before, /device:TPU:27 now
where the time goes in v1:
time: 142 us
  Pallas kernels  137 us (96%)
  local copies, waits for them, and re-layouts  3.05 us (2%)
    pallas_call x1, Pallas kernels, local_planes(): pl.pallas_call(functools.partial(planes_kernel, n, tok, cac, heads), out_...  137 us
    unnamed x1, local copies, waits for them, and re-layouts  3.05 us

profile of v1, /device:TPU:27, one launch (start us, length us, event | category | flops | bytes accessed | tf_op | source)
XLA Modules:
  0.0 141.7 jit_solution(573341726978478313)
XLA Ops:
  0.7 0.6 maximum_bitcast_fusion.inverse_ref
  1.3 137.3 %latent_attention.1 = bf16[64,16384]{1,0:T(8,128)(2,1)} custom-call(bf16[64,24576]{1,0:T(8,128)(2,1)} %q_hbm.1, bf16[64,576]{1,0:T(8,128)(2,1)} %kvn_hbm.1, bf16[32,576]{1,0:T(8,128)(2,1)} %kvc_hbm.1, bf16[512,1024]{1,0:T(8,128)(2,1)} %wk_hbm.1, bf16[512,1024]{1,0:T(8,128)(2,1)} %wv_hbm.1, f32[1,512]{1,0:T(1,128)} %bitcast.3, ...), custom_call_target="tpu_custom_call" | custom-call | tf_op jit(solution)/shard_map/latent_attention/pallas_call | solution.py:955
  138.6 3.0 %copy.10 = bf16[64,16384]{1,0:T(8,128)(2,1)} copy(bf16[64,16384]{1,0:T(8,128)(2,1)} %latent_attention.1) | data formatting | bytes 4194304
  (1 shorter events, 0.0 us)

commit v2 on v1

--- a/solution.py
+++ b/solution.py
@@ -404,8 +404,9 @@
 
 
 PLANES = 4
-EXTRA_END = 2
-EXTRA_MIDDLE = 1
+EXTRA_END = 3
+EXTRA_MIDDLE = 0
+EXTRA_FAR = 1
 
 
 def planes_kernel(
@@ -414,7 +415,7 @@
     out_hbm,
     qbuf, kvn, kvc, weights, latents, aux, keys, vals, bias, score_a, score_b, prob_a, prob_b, obuf,
     cos_ref, sin_ref,
-    local_sem, own_q_sem, own_out_sem, q_send, q_recv, kv_send, kv_recv, o_send, o_recv, w_send, w_recv,
+    local_sem, own_w_sem, own_q_sem, own_out_sem, q_send, q_recv, kv_send, kv_recv, o_send, o_recv, w_send, w_recv,
 ):
     me = lax.axis_index("seq")
     part = lax.axis_index("groups")
@@ -458,11 +459,18 @@
     own = [
         pltpu.make_async_copy(kvn_hbm, blk(kvn, me, tok), local_sem.at[0]),
         pltpu.make_async_copy(kvc_hbm, blk(kvc, me, cac), local_sem.at[1]),
-        pltpu.make_async_copy(wk_hbm, weights.at[0, 0], local_sem.at[2]),
-        pltpu.make_async_copy(wv_hbm, weights.at[0, 1], local_sem.at[3]),
     ]
     for copy in own:
         copy.start()
+
+    def own_w(which, i):
+        source = wv_hbm if which else wk_hbm
+        return pltpu.make_async_copy(cols(source, i, 2 * NOPE), weights.at[0, which, i], own_w_sem.at[which, i])
+
+    for which in range(2):
+        @pl.loop(0, pairs)
+        def _(i):
+            own_w(which, i).start()
 
     barrier = pltpu.get_barrier_semaphore()
 
@@ -493,6 +501,18 @@
             ),
         ]
 
+    near = {"seq": whole(1 - middle) * INNER + inner}
+    beyond = {"seq": whole(2) * INNER + inner}
+
+    def far_query(source):
+        return pltpu.make_async_remote_copy(
+            src_ref=blk(qbuf.at[PLANES], source, tok),
+            dst_ref=blk(qbuf.at[PLANES], source, tok),
+            send_sem=q_send.at[PLANES + 1, source],
+            recv_sem=q_recv.at[PLANES, source],
+            device_id=near,
+        )
+
     def q_copy(k, to_plane, to, source):
         columns = jnp.where(k == PLANES, whole(last), head_plane(k)) * INNER + to
         return pltpu.make_async_remote_copy(
@@ -503,23 +523,27 @@
             device_id={"seq": to_plane * INNER + to},
         )
 
-    def o_copy(k, to_plane, to, source):
+    def o_part(k, part_of, to):
+        return obuf.at[k, pl.ds(pl.multiple_of(to * tok, tok), tok), pl.ds(pl.multiple_of(part_of * ow // 2, 128), ow // 2)]
+
+    def o_copy(k, part_of, to_plane, to, source):
         columns = jnp.where(k == PLANES, whole(last), head_plane(k)) * INNER + source
         return pltpu.make_async_remote_copy(
-            src_ref=blk(obuf.at[k], to, tok),
-            dst_ref=cols(out_hbm, columns, ow),
-            send_sem=o_send.at[k, to],
-            recv_sem=o_recv.at[k, source],
+            src_ref=o_part(k, part_of, to),
+            dst_ref=cols(out_hbm, 2 * columns + part_of, ow // 2),
+            send_sem=o_send.at[k, part_of, to],
+            recv_sem=o_recv.at[k, part_of, source],
             device_id={"seq": to_plane * INNER + to},
         )
 
-    def own_out(k):
+    def own_out(k, part_of):
+        columns = head_plane(k) * INNER + inner
         return pltpu.make_async_copy(
-            blk(obuf.at[k], inner, tok), cols(out_hbm, head_plane(k) * INNER + inner, ow), own_out_sem.at[k]
+            o_part(k, part_of, inner), cols(out_hbm, 2 * columns + part_of, ow // 2), own_out_sem.at[k, part_of]
         )
 
     def w_chunk(k, which, i):
-        return weights.at[k, which, :, pl.ds(pl.multiple_of(i * 2 * NOPE, 128), 2 * NOPE)]
+        return weights.at[k, which, i]
 
     def w_copy(way, k, to_k, which, i, device):
         return pltpu.make_async_remote_copy(
@@ -530,9 +554,6 @@
             device_id=device,
         )
 
-    near = {"seq": whole(1 - middle) * INNER + inner}
-    beyond = {"seq": whole(2) * INNER + inner}
-
     def w_near(k, which, i):
         return w_copy(0, k, jnp.where(k == 0, 1, 2), which, i, near)
 
@@ -543,7 +564,7 @@
         return w_copy(2, k, k, piece, i, beside)
 
     def extras(k):
-        return jnp.where(mid, jnp.where(k == 1, EXTRA_END, jnp.where(k == 2, EXTRA_MIDDLE, 0)), 0)
+        return jnp.where(mid, jnp.where(k == 1, EXTRA_END, jnp.where(k == 2, EXTRA_MIDDLE, EXTRA_FAR)), 0)
 
     def for_own_weights(do):
         @pl.loop(0, pairs)
@@ -588,8 +609,11 @@
         for copy in kv_copies(0, me, exclusive(plane, j, PLANES) * INNER + inner, True):
             copy.start()
 
-    own[2].wait()
-    own[3].wait()
+    for which in range(2):
+        @pl.loop(0, pairs)
+        def _(i):
+            own_w(which, i).wait()
+
     for_own_weights(lambda copy: copy.start())
 
     across = plane * INNER + (inner + 2) % INNER
@@ -597,30 +621,48 @@
     own[0].wait()
     own[1].wait()
 
+    own_far_q = pltpu.make_async_copy(
+        cols(q_hbm, whole(last) * INNER + inner, qw), blk(qbuf.at[PLANES], inner, tok), local_sem.at[2]
+    )
+
+    @pl.when(end)
+    def _():
+        own_far_q.start()
+
     @pl.loop(0, steps)
     def _(k):
         own_q(k).start()
 
-    @pl.loop(0, PLANES)
-    def _(j):
+    def for_queries(k, do):
+        @pl.loop(1, INNER)
+        def _(i):
+            do(q_copy(k, plane, (inner + i) % INNER, inner))
+
+    def relay_kv(j):
         b = exclusive(plane, j, PLANES) * INNER + inner
-
-        @pl.when(j > 0)
-        def _():
-            for copy in kv_copies(0, b, twin, False):
-                copy.wait_recv()
-
         for copy in kv_copies(1, b, across, False):
             copy.start()
         for copy in kv_copies(2, b, twin, False):
             copy.start()
 
-    def for_queries(k, do):
-        @pl.loop(1, INNER)
-        def _(i):
-            do(q_copy(k, plane, (inner + i) % INNER, inner))
-
+    relay_kv(0)
     for_queries(0, lambda copy: copy.start())
+
+    @pl.loop(1, PLANES)
+    def _(j):
+        for copy in kv_copies(0, exclusive(plane, j, PLANES) * INNER + inner, twin, False):
+            copy.wait_recv()
+        relay_kv(j)
+
+    for_queries(1, lambda copy: copy.start())
+
+    @pl.when(end)
+    def _():
+        for_queries(PLANES, lambda copy: copy.start())
+
+    @pl.loop(2, steps)
+    def _(k):
+        for_queries(k, lambda copy: copy.start())
 
     tsize = math.gcd(T, 256)
     csize = math.gcd(C, 256)
@@ -641,6 +683,15 @@
         0.0, -1e30,
     )
 
+    def pass_on_near(i):
+        pass_on(1, i)
+
+        @pl.when(mid)
+        def _():
+            pass_on(2, i)
+
+    pass_on_near(0)
+
     @pl.loop(0, PLANES)
     def _(j):
         b = exclusive(plane, j, PLANES) * INNER + (inner + 2) % INNER
@@ -649,18 +700,7 @@
         for copy in kv_copies(2, b, twin, False):
             copy.start()
 
-    @pl.loop(1, steps)
-    def _(k):
-        for_queries(k, lambda copy: copy.start())
-
-    def for_far_queries(do):
-        @pl.loop(0, INNER)
-        def _(i):
-            do(q_copy(PLANES, whole(1), (inner + i) % INNER, inner))
-
-    @pl.when(end)
-    def _():
-        for_far_queries(lambda copy: copy.start())
+    pass_on_near(1)
 
     @pl.loop(0, heads)
     def _(h):
@@ -708,30 +748,32 @@
         cos_ref[at, :] = cos_ref[at, :] * scale
         sin_ref[at, :] = sin_ref[at, :] * scale
 
+    pass_on_near(2)
     size = math.gcd(C, rows)
 
-    def project(k, p):
-        across_k = pl.ds(pl.multiple_of(p * 2 * NOPE, 128), 2 * NOPE)
-        across_v = pl.ds(pl.multiple_of(p * 2 * VH, 128), 2 * VH)
-
-        top_plane = jnp.where(mid & (k == last), jnp.maximum(plane, whole(0)), plane)
-
-        @pl.loop(0, (C + (top_plane + 1) * rows) // size)
-        def _(i):
-            at = pl.ds(pl.multiple_of(i * size, size), size)
+    def project_rows(k, p, live):
+        lane = lax.broadcasted_iota(jnp.int32, (size, 128), 1)
+        for first in range(0, live, size):
+            at = slice(first, first + size)
             latent = latents[at, :]
             rest = aux[at, :]
-            lane = lax.broadcasted_iota(jnp.int32, (size, 128), 1)
-            pair = jnp.dot(latent, weights[k, 0, :, across_k], preferred_element_type=f32) * scale
+            pair = jnp.dot(latent, weights[k, 0, p], preferred_element_type=f32) * scale
             keys[2 * p, at, 0:128] = pair[:, :128].astype(bf16)
             turned = pltpu.roll(pair[:, 128:], 64, 1)
             keys[2 * p + 1, at, 0:128] = jnp.where(lane < ROPE, rest, turned).astype(bf16)
             keys[2 * p + 1, at, 128:256] = jnp.where(lane < ROPE, turned, rest).astype(bf16)
-            both = jnp.dot(latent, weights[k, 1, :, across_v], preferred_element_type=f32).astype(bf16)
+            both = jnp.dot(latent, weights[k, 1, p], preferred_element_type=f32).astype(bf16)
             vals[2 * p, at, 0:128] = both[:, :128]
             vals[2 * p + 1, at, 0:128] = both[:, 128:]
 
-    def attend(slot, first_row, live):
+    def project(k, p):
+        top_plane = jnp.where(mid & (k == last), jnp.maximum(plane, whole(0)), plane)
+        for s in range(PLANES):
+            @pl.when(top_plane == s)
+            def _():
+                project_rows(k, p, C + (s + 1) * rows)
+
+    def attend(slot, first_row, live, first_pair, last_pair):
         cut = live - rows
 
         def rotated(p):
@@ -775,10 +817,9 @@
             mixed = jnp.dot(probs[:, 0:live], vals[h, 0:live, :], preferred_element_type=f32)
             obuf[slot, :, pl.ds(pl.multiple_of(h * VH, VH), VH)] = (mixed[:, :VH] / mixed[:, VH:]).astype(bf16)
 
-        @pl.loop(0, pairs + 1)
-        def _(t):
-            p = jnp.minimum(t, pairs - 1)
-            done = jnp.maximum(t - 1, 0)
+        @pl.loop(first_pair, last_pair)
+        def _(p):
+            done = jnp.maximum(p - 1, first_pair)
             even, odd = rotated(p)
             score(even, 2 * p, score_a)
             soften(score_b, prob_b)
@@ -787,91 +828,150 @@
             mix(prob_b, 2 * done + 1)
             score(odd, 2 * p + 1, score_b)
 
-    @pl.loop(0, steps)
-    def _(k):
+        soften(score_b, prob_b)
+        mix(prob_a, 2 * last_pair - 2)
+        mix(prob_b, 2 * last_pair - 1)
+
+    def attend_plane(slot, s, first_pair, last_pair):
+        for plane_of in range(PLANES):
+            @pl.when(s == plane_of)
+            def _():
+                attend(slot, plane_of * rows, C + (plane_of + 1) * rows, first_pair, last_pair)
+
+    def other_kind(k, p):
+        w_copy(2, k, k, 1 - piece, p, beside).wait_recv()
+
+        @pl.when(mid & (k == 1) & (p >= pairs - EXTRA_FAR))
+        def _():
+            w_beyond(k, 1 - piece, p).start()
+
+    @pl.loop(0, jnp.where(end, 5, 7))
+    def _(turn):
+        j = turn - 1
+        late = j >= 4
+        k = jnp.where(turn == 0, 0, jnp.where(end, 1 + j // 2, jnp.where(late, last, 2 - j % 2)))
+        half = jnp.where(turn == 0, 0, jnp.where(end | late, j % 2, j // 2))
         far = mid & (k == last)
-
-        @pl.loop(0, pairs)
+        first_pair = half * (pairs // 2)
+        last_pair = jnp.where(turn == 0, pairs, first_pair + pairs // 2)
+
+        @pl.loop(first_pair, last_pair)
         def _(p):
             @pl.when(k > 0)
             def _():
-                @pl.when((k == 1) | (end & (k == 2)) | ((k == 3) & (p >= 2)))
+                other_kind(k, p)
+
+            project(k, p)
+
+        @pl.when(half == 0)
+        def _():
+            own_q(k).wait()
+
+            @pl.loop(1, INNER)
+            def _(i):
+                q_copy(k, plane, inner, (inner + i) % INNER).wait_recv()
+
+            @pl.when(far)
+            def _():
+                @pl.loop(0, INNER)
+                def _(i):
+                    far_query(i).wait_recv()
+
+        @pl.when(end & (turn == 3))
+        def _():
+            pass_on(2, 2)
+
+        @pl.loop(jnp.where(far, 0, 1), 2)
+        def _(item):
+            slot = jnp.where(item == 0, PLANES, k)
+            attend_plane(slot, jnp.where(item == 0, whole(0), plane), first_pair, last_pair)
+
+            @pl.loop(first_pair // (pairs // 2), last_pair // (pairs // 2))
+            def _(part_of):
+                @pl.when(item == 0)
                 def _():
-                    pass_on(k, p)
-
-                @pl.when(mid & (k == 1))
+                    @pl.loop(0, INNER)
+                    def _(i):
+                        o_copy(PLANES, part_of, whole(0), (inner + i) % INNER, inner).start()
+
+                @pl.when(item == 1)
                 def _():
-                    pass_on(2, p)
-
-                w_copy(2, k, k, 1 - piece, p, beside).wait_recv()
-
-            project(k, p)
-
-        @pl.when(mid & (k == 2))
-        def _():
-            pass_on(3, 0)
-            pass_on(3, 1)
-
-        own_q(k).wait()
-
-        @pl.loop(1, INNER)
-        def _(i):
-            q_copy(k, plane, inner, (inner + i) % INNER).wait_recv()
-
-        for s in range(PLANES):
-            @pl.when(plane == s)
+                    own_out(k, part_of).start()
+
+                    @pl.loop(1, INNER)
+                    def _(i):
+                        o_copy(k, part_of, plane, (inner + i) % INNER, inner).start()
+
+            @pl.when((item == 0) & (turn == 5))
             def _():
-                attend(k, s * rows, C + (s + 1) * rows)
-
-        own_out(k).start()
-
-        @pl.loop(1, INNER)
-        def _(i):
-            o_copy(k, plane, (inner + i) % INNER, inner).start()
-
-        @pl.when(far)
-        def _():
+                pass_on(3, 3)
+
+        @pl.when(turn == 0)
+        def _():
+            pass_on_near(3)
+
+        @pl.when(end & (turn > 0) & (turn < 4))
+        def _():
+            pass_on(2, jnp.where(turn == 3, 3, turn - 1))
+
+        @pl.when(mid & ((turn == 1) | (turn == 3) | (turn == 4)))
+        def _():
+            pass_on(3, turn // 2)
+
+        @pl.when(end & (turn == 1))
+        def _():
+            @pl.loop(1, INNER)
+            def _(i):
+                q_copy(PLANES, plane, inner, (inner + i) % INNER).wait_recv()
+
+            own_far_q.wait()
+
             @pl.loop(0, INNER)
             def _(i):
-                q_copy(PLANES, plane, inner, i).wait_recv()
-
-    for s in range(PLANES):
-        @pl.when(mid & (whole(0) == s))
-        def _():
-            attend(PLANES, s * rows, C + (s + 1) * rows)
-
-    def for_far_outputs(do):
+                far_query(i).start()
+
+    @pl.loop(0, 2)
+    def _(part_of):
+        @pl.loop(0, steps)
+        def _(k):
+            own_out(k, part_of).wait()
+
+            @pl.loop(1, INNER)
+            def _(i):
+                o_copy(k, part_of, plane, (inner + i) % INNER, inner).wait_send()
+                o_copy(k, part_of, plane, inner, (inner + i) % INNER).wait_recv()
+
+        @pl.when(mid)
+        def _():
+            @pl.loop(0, INNER)
+            def _(i):
+                o_copy(PLANES, part_of, whole(0), (inner + i) % INNER, inner).wait_send()
+
+        @pl.when(end)
+        def _():
+            @pl.loop(0, INNER)
+            def _(i):
+                o_copy(PLANES, part_of, plane, inner, i).wait_recv()
+
+    @pl.loop(0, steps)
+    def _(k):
+        for_queries(k, lambda copy: copy.wait_send())
+
+    @pl.when(end)
+    def _():
+        for_queries(PLANES, lambda copy: copy.wait_send())
+
         @pl.loop(0, INNER)
         def _(i):
-            do(o_copy(PLANES, whole(0), (inner + i) % INNER, inner))
+            far_query(i).wait_send()
+
+    for_own_weights(lambda copy: copy.wait_send())
 
     @pl.when(mid)
     def _():
-        for_far_outputs(lambda copy: copy.start())
-
-    @pl.loop(0, steps)
-    def _(k):
-        own_out(k).wait()
-        for_queries(k, lambda copy: copy.wait_send())
-
-        @pl.loop(1, INNER)
+        @pl.loop(pairs - EXTRA_FAR, pairs)
         def _(i):
-            o_copy(k, plane, (inner + i) % INNER, inner).wait_send()
-            o_copy(k, plane, inner, (inner + i) % INNER).wait_recv()
-
-    @pl.when(mid)
-    def _():
-        for_far_outputs(lambda copy: copy.wait_send())
-
-    @pl.when(end)
-    def _():
-        for_far_queries(lambda copy: copy.wait_send())
-
-        @pl.loop(0, INNER)
-        def _(i):
-            o_copy(PLANES, plane, inner, i).wait_recv()
-
-    for_own_weights(lambda copy: copy.wait_send())
+            w_beyond(1, 1 - piece, i).wait_send()
 
     @pl.loop(1, steps)
     def _(k):
@@ -961,7 +1061,7 @@
             pltpu.VMEM((PLANES + 1, rows, heads * WIDTH), bf16),
             pltpu.VMEM((T, LATENT + ROPE), bf16),
             pltpu.VMEM((C, LATENT + ROPE), bf16),
-            pltpu.VMEM((PLANES, 2, LATENT, heads * NOPE), bf16),
+            pltpu.VMEM((PLANES, 2, pairs, LATENT, 2 * NOPE), bf16),
             pltpu.VMEM((S, LATENT), bf16),
             pltpu.VMEM((S, 128), f32),
             pltpu.VMEM((heads, S, 256), bf16),
@@ -974,15 +1074,16 @@
             pltpu.VMEM((PLANES + 1, rows, heads * VH), bf16),
             pltpu.VMEM((T, 128), f32),
             pltpu.VMEM((T, 128), f32),
-            dma((4,)),
+            dma((3,)),
+            dma((2, pairs)),
             dma((PLANES,)),
-            dma((PLANES,)),
-            dma((PLANES + 1, INNER)),
+            dma((PLANES, 2)),
+            dma((PLANES + 2, INNER)),
             dma((PLANES + 1, INNER)),
             dma((6, n)),
             dma((2, n)),
-            dma((PLANES + 1, INNER)),
-            dma((PLANES + 1, INNER)),
+            dma((PLANES + 1, 2, INNER)),
+            dma((PLANES + 1, 2, INNER)),
             dma((3, PLANES, 2, pairs)),
             dma((PLANES, 2, pairs)),
         ],

time: 142 us -> 96.3 us (0.68)
  the two profiles are of different devices: /device:TPU:27 before, /device:TPU:17 now
where the time goes in v2:
time: 96.3 us; the launch traced here: 96.1 us
  Pallas kernels  91.8 us (95%)
  local copies, waits for them, and re-layouts  3.05 us (3%)
    pallas_call x1, Pallas kernels, local_planes(): pl.pallas_call(functools.partial(planes_kernel, n, tok, cac, heads), out_...  91.8 us
    unnamed x1, local copies, waits for them, and re-layouts  3.05 us

profile of v2, /device:TPU:17, one launch (start us, length us, event | category | flops | bytes accessed | tf_op | source)
XLA Modules:
  0.0 96.1 jit_solution(9900530274899204906)
XLA Ops:
  0.7 0.6 maximum_bitcast_fusion.inverse_ref
  1.3 91.8 %latent_attention.1 = bf16[64,16384]{1,0:T(8,128)(2,1)} custom-call(bf16[64,24576]{1,0:T(8,128)(2,1)} %q_hbm.1, bf16[64,576]{1,0:T(8,128)(2,1)} %kvn_hbm.1, bf16[32,576]{1,0:T(8,128)(2,1)} %kvc_hbm.1, bf16[512,1024]{1,0:T(8,128)(2,1)} %wk_hbm.1, bf16[512,1024]{1,0:T(8,128)(2,1)} %wv_hbm.1, f32[1,512]{1,0:T(1,128)} %bitcast.3, ...), custom_call_target="tpu_custom_call" | custom-call | tf_op jit(solution)/shard_map/latent_attention/pallas_call | solution.py:1055
  93.0 3.0 %copy.10 = bf16[64,16384]{1,0:T(8,128)(2,1)} copy(bf16[64,16384]{1,0:T(8,128)(2,1)} %latent_attention.1) | data formatting | bytes 4194304
  (1 shorter events, 0.0 us)

commit v3 on v2

--- a/solution.py
+++ b/solution.py
@@ -566,6 +566,8 @@
     def extras(k):
         return jnp.where(mid, jnp.where(k == 1, EXTRA_END, jnp.where(k == 2, EXTRA_MIDDLE, EXTRA_FAR)), 0)
 
+    late_pair = pairs - 2
+
     def for_own_weights(do):
         @pl.loop(0, pairs)
         def _(i):
@@ -579,7 +581,9 @@
         def _():
             @pl.loop(pairs - EXTRA_END, pairs)
             def _(i):
-                do(w_near(0, 1 - piece, i))
+                @pl.when(i != late_pair)
+                def _():
+                    do(w_near(0, 1 - piece, i))
 
         @pl.when(mid)
         def _():
@@ -638,31 +642,33 @@
         def _(i):
             do(q_copy(k, plane, (inner + i) % INNER, inner))
 
-    def relay_kv(j):
-        b = exclusive(plane, j, PLANES) * INNER + inner
+    def relay_kv(p):
+        b = p * INNER + inner
         for copy in kv_copies(1, b, across, False):
             copy.start()
         for copy in kv_copies(2, b, twin, False):
             copy.start()
 
-    relay_kv(0)
+    relay_kv(plane)
     for_queries(0, lambda copy: copy.start())
 
     @pl.loop(1, PLANES)
     def _(j):
-        for copy in kv_copies(0, exclusive(plane, j, PLANES) * INNER + inner, twin, False):
+        p = exclusive(plane, j, PLANES)
+        for copy in kv_copies(0, p * INNER + inner, twin, False):
             copy.wait_recv()
-        relay_kv(j)
-
-    for_queries(1, lambda copy: copy.start())
+        relay_kv(p)
 
     @pl.when(end)
     def _():
         for_queries(PLANES, lambda copy: copy.start())
-
-    @pl.loop(2, steps)
-    def _(k):
-        for_queries(k, lambda copy: copy.start())
+        for_queries(1, lambda copy: copy.start())
+        for_queries(2, lambda copy: copy.start())
+
+    @pl.when(mid)
+    def _():
+        for k in (2, 1, 3):
+            for_queries(k, lambda copy: copy.start())
 
     tsize = math.gcd(T, 256)
     csize = math.gcd(C, 256)
@@ -839,27 +845,29 @@
                 attend(slot, plane_of * rows, C + (plane_of + 1) * rows, first_pair, last_pair)
 
     def other_kind(k, p):
-        w_copy(2, k, k, 1 - piece, p, beside).wait_recv()
-
-        @pl.when(mid & (k == 1) & (p >= pairs - EXTRA_FAR))
-        def _():
-            w_beyond(k, 1 - piece, p).start()
+        return w_copy(2, k, k, 1 - piece, p, beside)
 
     @pl.loop(0, jnp.where(end, 5, 7))
     def _(turn):
-        j = turn - 1
-        late = j >= 4
-        k = jnp.where(turn == 0, 0, jnp.where(end, 1 + j // 2, jnp.where(late, last, 2 - j % 2)))
-        half = jnp.where(turn == 0, 0, jnp.where(end | late, j % 2, j // 2))
+        ends_k = 1 + (turn - 1) // 2
+        mids_k = jnp.where(turn <= 2, 2, jnp.where((turn == 3) | (turn == 6), 1, last))
+        k = jnp.where(turn == 0, 0, jnp.where(end, ends_k, mids_k))
+        ends_half = (turn + 1) % 2
+        mids_half = jnp.where((turn == 2) | (turn >= 5), 1, 0)
+        half = jnp.where(turn == 0, 0, jnp.where(end, ends_half, mids_half))
         far = mid & (k == last)
         first_pair = half * (pairs // 2)
         last_pair = jnp.where(turn == 0, pairs, first_pair + pairs // 2)
 
+        @pl.when(mid & (turn == 5))
+        def _():
+            pass_on(3, 3)
+
         @pl.loop(first_pair, last_pair)
         def _(p):
-            @pl.when(k > 0)
+            @pl.when((k > 0) & ~(mid & (k == 1) & (p >= pairs - EXTRA_FAR)))
             def _():
-                other_kind(k, p)
+                other_kind(k, p).wait_recv()
 
             project(k, p)
 
@@ -871,30 +879,36 @@
             def _(i):
                 q_copy(k, plane, inner, (inner + i) % INNER).wait_recv()
 
-            @pl.when(far)
+        @pl.when(turn == 0)
+        def _():
+            pass_on_near(3)
+
+        @pl.when(end & (turn == 3))
+        def _():
+            pass_on(2, 2)
+
+        @pl.loop(jnp.where(far, 0, 1), 2)
+        def _(item):
+            far_item = far & (item == jnp.where(turn == 5, 0, 1))
+
+            @pl.when(far_item & (turn == 4))
             def _():
                 @pl.loop(0, INNER)
                 def _(i):
                     far_query(i).wait_recv()
 
-        @pl.when(end & (turn == 3))
-        def _():
-            pass_on(2, 2)
-
-        @pl.loop(jnp.where(far, 0, 1), 2)
-        def _(item):
-            slot = jnp.where(item == 0, PLANES, k)
-            attend_plane(slot, jnp.where(item == 0, whole(0), plane), first_pair, last_pair)
+            slot = jnp.where(far_item, PLANES, k)
+            attend_plane(slot, jnp.where(far_item, whole(0), plane), first_pair, last_pair)
 
             @pl.loop(first_pair // (pairs // 2), last_pair // (pairs // 2))
             def _(part_of):
-                @pl.when(item == 0)
+                @pl.when(far_item)
                 def _():
                     @pl.loop(0, INNER)
                     def _(i):
                         o_copy(PLANES, part_of, whole(0), (inner + i) % INNER, inner).start()
 
-                @pl.when(item == 1)
+                @pl.when(~far_item)
                 def _():
                     own_out(k, part_of).start()
 
@@ -902,23 +916,22 @@
                     def _(i):
                         o_copy(k, part_of, plane, (inner + i) % INNER, inner).start()
 
-            @pl.when((item == 0) & (turn == 5))
-            def _():
-                pass_on(3, 3)
-
-        @pl.when(turn == 0)
-        def _():
-            pass_on_near(3)
-
         @pl.when(end & (turn > 0) & (turn < 4))
         def _():
             pass_on(2, jnp.where(turn == 3, 3, turn - 1))
 
-        @pl.when(mid & ((turn == 1) | (turn == 3) | (turn == 4)))
-        def _():
-            pass_on(3, turn // 2)
-
-        @pl.when(end & (turn == 1))
+        @pl.when(mid & ((turn < 2) | (turn == 3)))
+        def _():
+            pass_on(3, jnp.where(turn == 3, 2, turn))
+
+        @pl.when(mid & (turn == 1))
+        def _():
+            @pl.loop(pairs - EXTRA_FAR, pairs)
+            def _(p):
+                other_kind(1, p).wait_recv()
+                w_beyond(1, 1 - piece, p).start()
+
+        @pl.when(end & (turn == 0))
         def _():
             @pl.loop(1, INNER)
             def _(i):
@@ -929,6 +942,8 @@
             @pl.loop(0, INNER)
             def _(i):
                 far_query(i).start()
+
+            w_near(0, 1 - piece, late_pair).start()
 
     @pl.loop(0, 2)
     def _(part_of):
@@ -964,6 +979,8 @@
         @pl.loop(0, INNER)
         def _(i):
             far_query(i).wait_send()
+
+        w_near(0, 1 - piece, late_pair).wait_send()
 
     for_own_weights(lambda copy: copy.wait_send())
 

time: 96.3 us -> 94.4 us (0.980)
  Pallas kernels: 91.8 us -> 89.9 us
    pallas_call x1, Pallas kernels: 91.8 us -> 89.9 us  [local_planes(): pl.pallas_call(functools.partial(planes_kernel, n, tok, cac, heads), out_...]
where the time goes in v3:
time: 94.4 us; the launch traced here: 94.2 us
  Pallas kernels  89.9 us (95%)
  local copies, waits for them, and re-layouts  3.05 us (3%)
    pallas_call x1, Pallas kernels, local_planes(): pl.pallas_call(functools.partial(planes_kernel, n, tok, cac, heads), out_...  89.9 us
    unnamed x1, local copies, waits for them, and re-layouts  3.05 us

profile of v3, /device:TPU:17, one launch (start us, length us, event | category | flops | bytes accessed | tf_op | source)
XLA Modules:
  0.0 94.2 jit_solution(9354376006038229107)
XLA Ops:
  0.7 0.6 maximum_bitcast_fusion.inverse_ref
  1.3 89.9 %latent_attention.1 = bf16[64,16384]{1,0:T(8,128)(2,1)} custom-call(bf16[64,24576]{1,0:T(8,128)(2,1)} %q_hbm.1, bf16[64,576]{1,0:T(8,128)(2,1)} %kvn_hbm.1, bf16[32,576]{1,0:T(8,128)(2,1)} %kvc_hbm.1, bf16[512,1024]{1,0:T(8,128)(2,1)} %wk_hbm.1, bf16[512,1024]{1,0:T(8,128)(2,1)} %wv_hbm.1, f32[1,512]{1,0:T(1,128)} %bitcast.3, ...), custom_call_target="tpu_custom_call" | custom-call | tf_op jit(solution)/shard_map/latent_attention/pallas_call | solution.py:1072
  91.2 3.0 %copy.10 = bf16[64,16384]{1,0:T(8,128)(2,1)} copy(bf16[64,16384]{1,0:T(8,128)(2,1)} %latent_attention.1) | data formatting | bytes 4194304
  (1 shorter events, 0.0 us)

commit v4 on v3

--- a/solution.py
+++ b/solution.py
@@ -650,14 +650,14 @@
             copy.start()
 
     relay_kv(plane)
-    for_queries(0, lambda copy: copy.start())
-
     @pl.loop(1, PLANES)
     def _(j):
         p = exclusive(plane, j, PLANES)
         for copy in kv_copies(0, p * INNER + inner, twin, False):
             copy.wait_recv()
         relay_kv(p)
+
+    for_queries(0, lambda copy: copy.start())
 
     @pl.when(end)
     def _():

time: 94.4 us -> 94.4 us (level)
  no operation moved by 1% of the time
where the time goes in v4:
time: 94.4 us; the launch traced here: 94.2 us
  Pallas kernels  89.9 us (95%)
  local copies, waits for them, and re-layouts  3.05 us (3%)
    pallas_call x1, Pallas kernels, local_planes(): pl.pallas_call(functools.partial(planes_kernel, n, tok, cac, heads), out_...  89.9 us
    unnamed x1, local copies, waits for them, and re-layouts  3.05 us

profile of v4, /device:TPU:17, one launch (start us, length us, event | category | flops | bytes accessed | tf_op | source)
XLA Modules:
  0.0 94.2 jit_solution(16501358343878146738)
XLA Ops:
  0.7 0.6 maximum_bitcast_fusion.inverse_ref
  1.3 89.9 %latent_attention.1 = bf16[64,16384]{1,0:T(8,128)(2,1)} custom-call(bf16[64,24576]{1,0:T(8,128)(2,1)} %q_hbm.1, bf16[64,576]{1,0:T(8,128)(2,1)} %kvn_hbm.1, bf16[32,576]{1,0:T(8,128)(2,1)} %kvc_hbm.1, bf16[512,1024]{1,0:T(8,128)(2,1)} %wk_hbm.1, bf16[512,1024]{1,0:T(8,128)(2,1)} %wv_hbm.1, f32[1,512]{1,0:T(1,128)} %bitcast.3, ...), custom_call_target="tpu_custom_call" | custom-call | tf_op jit(solution)/shard_map/latent_attention/pallas_call | solution.py:1072
  91.2 3.0 %copy.10 = bf16[64,16384]{1,0:T(8,128)(2,1)} copy(bf16[64,16384]{1,0:T(8,128)(2,1)} %latent_attention.1) | data formatting | bytes 4194304
  (1 shorter events, 0.0 us)
